TPU v7x, 32 devices: a whole 2x2x4 slice. The times are simulated.
32 devices in a mesh: expert: 4 (over z), shard: 8 (over y, x, core).
Axes of the slice: x: 2, y: 2, z: 4, core: 2. Of those that a mesh axis runs over, the one named last changes fastest.
Arguments:
- master_gate: float32 [64, 2048, 1408], P('expert', 'shard'), may hold values from -0.1875 to 0.1875
- master_up: float32 [64, 2048, 1408], P('expert', 'shard'), may hold values from -0.1875 to 0.1875
- router_weight: float32 [2048, 64], P('shard', 'expert'), may hold values from -0.125 to 0.125
- router_gain: float32 [2048], P('shard'), may hold values from 0.25 to 1.75
Outputs:
- final_gate: bfloat16 [64, 2048, 1408], P('expert', None, 'shard')
- final_up: bfloat16 [64, 2048, 1408], P('expert', None, 'shard')
- scale_gate: float32 [64, 1408], P('expert', 'shard')
- scale_up: float32 [64, 1408], P('expert', 'shard')
- serve_router: bfloat16 [2048, 64], replicated
All inputs are finite; a program needn't handle non-finite values.
Results may differ from a plain program's by a relative error of at most 0.001.
Values may be sent and summed in bfloat16 or wider, within the bound.
A program may use at most 192 MiB of HBM per device.

v0:
```python
import jax
import jax.numpy as jnp
from jax import lax
from jax.sharding import PartitionSpec as P


def local(master_gate, master_up, router_weight, router_gain):
    total_gate, total_up = lax.psum(
        (jnp.sum(master_gate * master_gate, axis=1), jnp.sum(master_up * master_up, axis=1)),
        "shard",
    )
    scale_gate = jnp.sqrt(total_gate)
    scale_up = jnp.sqrt(total_up)
    narrow_gate, narrow_up = (
        (master_gate / jnp.expand_dims(scale_gate, 1)).astype(jnp.bfloat16),
        (master_up / jnp.expand_dims(scale_up, 1)).astype(jnp.bfloat16),
    )
    final_gate, final_up = (
        lax.all_to_all(narrow_gate, "shard", split_axis=2, concat_axis=1, tiled=True),
        lax.all_to_all(narrow_up, "shard", split_axis=2, concat_axis=1, tiled=True),
    )
    scale_gate = lax.dynamic_slice_in_dim(
        scale_gate, lax.axis_index("shard") * final_gate.shape[2], final_gate.shape[2], axis=1
    )
    scale_up = lax.dynamic_slice_in_dim(
        scale_up, lax.axis_index("shard") * final_up.shape[2], final_up.shape[2], axis=1
    )
    part_router = (router_weight * router_gain[:, None]).astype(jnp.bfloat16)
    row_router = lax.all_gather(part_router, "shard", axis=0, tiled=True)
    serve_router = lax.all_gather(row_router, "expert", axis=1, tiled=True)
    return (final_gate, final_up, scale_gate, scale_up, serve_router)


def solution(mesh):
    in_specs = (
        P("expert", "shard", None),
        P("expert", "shard", None),
        P("shard", "expert"),
        P("shard"),
    )
    out_specs = (
        P("expert", None, "shard"),
        P("expert", None, "shard"),
        P("expert", "shard"),
        P("expert", "shard"),
        P(),
    )
    return jax.shard_map(local, mesh=mesh, in_specs=in_specs, out_specs=out_specs, check_vma=False)
```

profile of v0, /device:TPU:0, one launch (start us, length us, event | category | flops | bytes accessed | tf_op | source)
XLA Modules:
  0.0 445.2 jit_solution(13781813590717320649)
XLA Ops:
  7.2 0.0 all-reduce.3.cloned.1.call-start
  7.2 15.8 %multiply_reduce_fusion = (f32[16,1408]{1,0:T(8,128)}, f32[16,1408]{1,0:T(8,128)}) fusion(f32[16,256,1408]{2,1,0:T(8,128)} %param.5, f32[16,256,1408]{2,1,0:T(8,128)} %param.4), kind=kLoop, calls=%fused_computation.1 | loop fusion | flops 23023616 | bytes 46317568 | tf_op jit(solution)/shard_map/reduce_sum | solution.py:9
  23.0 0.0 all-reduce.3.cloned.1.call-update
  23.1 23.7 %copy.22 = f32[16,256,1408]{1,0,2:T(8,128)} copy(f32[16,256,1408]{2,1,0:T(8,128)} %param.5) | data formatting | bytes 46137344 | tf_op args[1]
  46.8 32.3 %all-reduce.3.cloned.1.call-done = (f32[16,1408]{1,0:T(8,128)}, f32[16,1408]{1,0:T(8,128)}) async-done(((f32[16,1408]{1,0:T(8,128)}, f32[16,1408]{1,0:T(8,128)}), (f32[16,1408]{1,0:T(8,128)}, f32[16,1408]{1,0:T(8,128)})) %all-reduce.3.cloned.1.call-update) | async-done | bytes 180240 | tf_op jit(solution)/shard_map/psum | solution.py:8
  79.0 0.9 sqrt.7
  80.0 0.3 copy.21
  80.2 14.2 %divide_convert_fusion = bf16[16,256,1408]{1,0,2:T(8,128)(2,1)} fusion(f32[16,256,1408]{1,0,2:T(8,128)} %copy.22, f32[16,1408]{0,1:T(8,128)S(1)} %copy.21), kind=kLoop, calls=%fused_computation | loop fusion | flops 11534336 | bytes 34693120 | tf_op jit(solution)/shard_map/convert_element_type | solution.py:16
  94.4 5.2 %all-to-all-start.1 = ((bf16[16,256,1408]{1,0,2:T(8,128)(2,1)}), bf16[16,256,1408]{1,0,2:T(8,128)(2,1)}, u32[]{:S(2)}, u32[]{:S(2)}) async-start(bf16[16,256,1408]{1,0,2:T(8,128)(2,1)} %divide_convert_fusion), calls=%async_computation.1 | async-start | bytes 23068672 | tf_op jit(solution)/shard_map/all_to_all | solution.py:20
  99.7 0.0 copy-start
  99.7 23.7 %copy.18 = f32[16,256,1408]{1,0,2:T(8,128)} copy(f32[16,256,1408]{2,1,0:T(8,128)} %param.4) | data formatting | bytes 46137344 | tf_op args[0]
  123.4 0.0 copy-done
  123.4 0.3 copy.17
  123.7 0.0 copy-start.1
  123.7 0.0 copy-start.2
  123.7 14.2 %divide_convert_fusion.1 = bf16[16,256,1408]{1,0,2:T(8,128)(2,1)} fusion(f32[16,256,1408]{1,0,2:T(8,128)} %copy.18, f32[16,1408]{0,1:T(8,128)S(1)} %copy.17), kind=kLoop, calls=%fused_computation.2 | loop fusion | flops 11534336 | bytes 34693120 | tf_op jit(solution)/shard_map/convert_element_type | solution.py:15
  138.0 89.5 %all-to-all-done.1 = bf16[16,256,1408]{1,0,2:T(8,128)(2,1)} async-done(((bf16[16,256,1408]{1,0,2:T(8,128)(2,1)}), bf16[16,256,1408]{1,0,2:T(8,128)(2,1)}, u32[]{:S(2)}, u32[]{:S(2)}) %all-to-all-start.1) | async-done | bytes 11534368 | tf_op jit(solution)/shard_map/all_to_all | solution.py:20
  227.4 5.3 %all-to-all-start = ((bf16[16,256,1408]{1,0,2:T(8,128)(2,1)}), bf16[16,256,1408]{1,0,2:T(8,128)(2,1)}, u32[]{:S(2)}, u32[]{:S(2)}) async-start(bf16[16,256,1408]{1,0,2:T(8,128)(2,1)} %divide_convert_fusion.1), calls=%async_computation | async-start | bytes 23068672 | tf_op jit(solution)/shard_map/all_to_all | solution.py:19
  232.7 0.0 copy-done.1
  232.7 0.0 copy-done.2
  232.7 130.9 %all_gather.6 = bf16[2048,16]{0,1:T(8,128)(2,1)S(1)} all-gather(bf16[256,16]{0,1:T(8,128)(2,1)S(1)} %multiply_convert_fusion), channel_id=1, replica_groups=mesh['expert'=4,'shard'=8] {'shard'}, dimensions={0}, use_global_device_ids=true | all-gather | bytes 73728 | tf_op jit(solution)/shard_map/all_gather | solution.py:29
  363.6 14.0 %all_gather.7 = bf16[2048,64]{0,1:T(8,128)(2,1)S(1)} all-gather(bf16[2048,16]{0,1:T(8,128)(2,1)S(1)} %all_gather.6), channel_id=1, replica_groups=mesh['expert'=4,'shard'=8] {'expert'}, dimensions={1}, use_global_device_ids=true | all-gather | bytes 327680 | tf_op jit(solution)/shard_map/all_gather | solution.py:30
  377.6 0.7 constant_dynamic-slice_fusion
  378.3 0.7 constant_dynamic-slice_fusion.1
  379.0 11.4 %copy.24 = bf16[16,8,256,176]{2,1,3,0:T(8,128)(2,1)} copy(bf16[16,8,256,176]{2,0,3,1:T(8,128)(2,1)} %bitcast.5) | data formatting | bytes 23068672 | tf_op jit(solution)/shard_map/all_to_all | solution.py:20
  390.4 18.0 %all_to_all.33 = bf16[16,2048,176]{1,2,0:T(8,128)(2,1)} reshape(bf16[16,8,256,176]{2,1,3,0:T(8,128)(2,1)} %copy.24) | data formatting | bytes 23068672 | tf_op jit(solution)/shard_map/all_to_all | solution.py:20
  408.3 0.0 all-to-all-done
  408.3 11.4 %copy.20 = bf16[16,8,256,176]{2,1,3,0:T(8,128)(2,1)} copy(bf16[16,8,256,176]{2,0,3,1:T(8,128)(2,1)} %bitcast.2) | data formatting | bytes 23068672 | tf_op jit(solution)/shard_map/all_to_all | solution.py:19
  419.7 18.0 %all_to_all.29 = bf16[16,2048,176]{1,2,0:T(8,128)(2,1)} reshape(bf16[16,8,256,176]{2,1,3,0:T(8,128)(2,1)} %copy.20) | data formatting | bytes 23068672 | tf_op jit(solution)/shard_map/all_to_all | solution.py:19
  437.7 0.7 copy.30
  (2 shorter events, 0.0 us)
Async XLA Ops:
  7.2 71.9 %all-reduce.3.cloned.1.call-start = ((), (), s32[]{:S(2)}) async-start(), calls=%async_computation.2 | async-start | bytes 360448 | tf_op jit(solution)/shard_map/psum | solution.py:8
  94.4 133.0 %all-to-all-start.1 = ((bf16[16,256,1408]{1,0,2:T(8,128)(2,1)}), bf16[16,256,1408]{1,0,2:T(8,128)(2,1)}, u32[]{:S(2)}, u32[]{:S(2)}) async-start(bf16[16,256,1408]{1,0,2:T(8,128)(2,1)} %divide_convert_fusion), calls=%async_computation.1 | async-start | bytes 23068672 | tf_op jit(solution)/shard_map/all_to_all | solution.py:20
  99.7 23.7 %copy-start = (f32[16,1408]{1,0:T(8,128)S(1)}, f32[16,1408]{1,0:T(8,128)}, u32[]{:S(2)}) copy-start(f32[16,1408]{1,0:T(8,128)} %get-tuple-element.5) | copy-start | bytes 270340
  123.7 109.0 %copy-start.1 = (f32[256,16]{0,1:T(8,128)S(1)}, f32[256,16]{0,1:T(8,128)}, u32[]{:S(2)}) copy-start(f32[256,16]{0,1:T(8,128)} %param.6) | copy-start | bytes 49156
  123.7 109.0 %copy-start.2 = (f32[256]{0:T(256)S(1)}, f32[256]{0:T(256)}, u32[]{:S(2)}) copy-start(f32[256]{0:T(256)} %param.7) | copy-start | bytes 3076
  227.4 180.9 %all-to-all-start = ((bf16[16,256,1408]{1,0,2:T(8,128)(2,1)}), bf16[16,256,1408]{1,0,2:T(8,128)(2,1)}, u32[]{:S(2)}, u32[]{:S(2)}) async-start(bf16[16,256,1408]{1,0,2:T(8,128)(2,1)} %divide_convert_fusion.1), calls=%async_computation | async-start | bytes 23068672 | tf_op jit(solution)/shard_map/all_to_all | solution.py:19
Sparse Core Ops, SparseCore 0:
  23.2 55.8 all-reduce.2
where the time goes:
time: 447 us; the launch traced here: 445 us
  blocking collectives  145 us (32%)
  waiting for transfers between devices  122 us (27%)
  local copies, waits for them, and re-layouts  110 us (25%)
  other arithmetic  44.3 us (10%)
  between operations  14.1 us (3%)
  starting transfers between devices  10.5 us (2%)
    all_gather x1, blocking collectives, local(): row_router = lax.all_gather(part_router, 'shard', axis=0, tiled=True)  131 us
    all_to_all x1, waiting for transfers between devices, local(): lax.all_to_all(narrow_up, 'shard', split_axis=2, concat_axis=1, tiled=True)  89.5 us
    unnamed x9, local copies, waits for them, and re-layouts  48.1 us
    psum x1, waiting for transfers between devices, local(): lax.psum((jnp.sum(master_gate * master_gate, axis=1), jnp.sum(master_up *...  32.3 us
    all_to_all x2, local copies, waits for them, and re-layouts, local(): lax.all_to_all(narrow_gate, 'shard', split_axis=2, concat_axis=1, tiled=T...  29.3 us
    all_to_all x2, local copies, waits for them, and re-layouts, local(): lax.all_to_all(narrow_up, 'shard', split_axis=2, concat_axis=1, tiled=True)  29.3 us
    reduce_sum x1, other arithmetic, local(): jnp.sum(master_up * master_up, axis=1)  15.8 us
    convert_element_type x1, other arithmetic, local(): (master_up / jnp.expand_dims(scale_up, 1)).astype(jnp.bfloat16)  14.2 us
  transfers between devices with their start and end apart: 3, of which 2 were waited for; matrix products, arithmetic and copies ran while one was open for 17% of the time, Pallas kernels for 0%

commit v1 on v0

--- a/solution.py
+++ b/solution.py
@@ -26,7 +26,13 @@
         scale_up, lax.axis_index("shard") * final_up.shape[2], final_up.shape[2], axis=1
     )
     part_router = (router_weight * router_gain[:, None]).astype(jnp.bfloat16)
-    row_router = lax.all_gather(part_router, "shard", axis=0, tiled=True)
+    size = lax.axis_size("shard")
+    held, blocks = (part_router, [part_router])
+    for _ in range(size - 1):
+        held = lax.ppermute(held, "shard", [(i, (i + 1) % size) for i in range(size)])
+        blocks.insert(0, held)
+    merged = jnp.concatenate(blocks, axis=0)
+    row_router = jnp.roll(merged, (lax.axis_index("shard") + 1) * part_router.shape[0], axis=0)
     serve_router = lax.all_gather(row_router, "expert", axis=1, tiled=True)
     return (final_gate, final_up, scale_gate, scale_up, serve_router)
 

time: 447 us -> 468 us (1.047)
  waiting for transfers between devices: 122 us -> 272 us
  blocking collectives: 145 us -> 14.4 us
    ppermute x0 -> x7, waiting for transfers between devices: none -> 151 us  [local(): lax.ppermute(held, 'shard', [(i, (i + 1) % size) for i in range(size)])]
    all_gather x1 -> x0, blocking collectives: 131 us -> none  [local(): row_router = lax.all_gather(part_router, 'shard', axis=0, tiled=True)]
    all_to_all x1, waiting for transfers between devices: 89.5 us -> 0.01 us  [local(): lax.all_to_all(narrow_up, 'shard', split_axis=2, concat_axis=1, tiled=True)]
    all_to_all x1, waiting for transfers between devices: 0.01 us -> 89.5 us  [local(): lax.all_to_all(narrow_gate, 'shard', split_axis=2, concat_axis=1, tiled=T...]
    unnamed x9 -> x23, local copies, waits for them, and re-layouts: 48.1 us -> 48.1 us
  transfers between devices with their start and end apart: 3 -> 10, of which waited for: 2 -> 9; matrix products, arithmetic and copies ran while one was open for 17% -> 16% of each run, Pallas kernels for 0% -> 0%
where the time goes in v1:
time: 468 us; the launch traced here: 466 us
  waiting for transfers between devices  272 us (58%)
  local copies, waits for them, and re-layouts  110 us (24%)
  other arithmetic  44.3 us (9%)
  blocking collectives  14.4 us (3%)
  between operations  14.2 us (3%)
  starting transfers between devices  11 us (2%)
    ppermute x7, waiting for transfers between devices, local(): lax.ppermute(held, 'shard', [(i, (i + 1) % size) for i in range(size)])  151 us
    all_to_all x1, waiting for transfers between devices, local(): lax.all_to_all(narrow_gate, 'shard', split_axis=2, concat_axis=1, tiled=T...  89.5 us
    unnamed x23, local copies, waits for them, and re-layouts  48.1 us
    psum x1, waiting for transfers between devices, local(): lax.psum((jnp.sum(master_gate * master_gate, axis=1), jnp.sum(master_up *...  32.3 us
    all_to_all x2, local copies, waits for them, and re-layouts, local(): lax.all_to_all(narrow_up, 'shard', split_axis=2, concat_axis=1, tiled=True)  29.3 us
    all_to_all x2, local copies, waits for them, and re-layouts, local(): lax.all_to_all(narrow_gate, 'shard', split_axis=2, concat_axis=1, tiled=T...  29.3 us
    reduce_sum x1, other arithmetic, local(): jnp.sum(master_up * master_up, axis=1)  15.8 us
    all_gather x1, blocking collectives, local(): serve_router = lax.all_gather(row_router, 'expert', axis=1, tiled=True)  14.4 us
  transfers between devices with their start and end apart: 10, of which 9 were waited for; matrix products, arithmetic and copies ran while one was open for 16% of the time, Pallas kernels for 0%

profile of v1, /device:TPU:0, one launch (start us, length us, event | category | flops | bytes accessed | tf_op | source)
XLA Modules:
  0.0 465.9 jit_solution(12689539021334637205)
XLA Ops:
  7.2 0.0 all-reduce.3.cloned.1.call-start
  7.2 15.8 %multiply_reduce_fusion = (f32[16,1408]{1,0:T(8,128)}, f32[16,1408]{1,0:T(8,128)}) fusion(f32[16,256,1408]{2,1,0:T(8,128)} %param.5, f32[16,256,1408]{2,1,0:T(8,128)} %param.4), kind=kLoop, calls=%fused_computation.1 | loop fusion | flops 23023616 | bytes 46317568 | tf_op jit(solution)/shard_map/reduce_sum | solution.py:9
  23.0 0.0 all-reduce.3.cloned.1.call-update
  23.1 23.7 %copy.18 = f32[16,256,1408]{1,0,2:T(8,128)} copy(f32[16,256,1408]{2,1,0:T(8,128)} %param.4) | data formatting | bytes 46137344 | tf_op args[0]
  46.8 32.3 %all-reduce.3.cloned.1.call-done = (f32[16,1408]{1,0:T(8,128)}, f32[16,1408]{1,0:T(8,128)}) async-done(((f32[16,1408]{1,0:T(8,128)}, f32[16,1408]{1,0:T(8,128)}), (f32[16,1408]{1,0:T(8,128)}, f32[16,1408]{1,0:T(8,128)})) %all-reduce.3.cloned.1.call-update) | async-done | bytes 180240 | tf_op jit(solution)/shard_map/psum | solution.py:8
  79.0 0.9 sqrt.6
  80.0 0.3 copy.17
  80.2 14.2 %divide_convert_fusion.1 = bf16[16,256,1408]{1,0,2:T(8,128)(2,1)} fusion(f32[16,256,1408]{1,0,2:T(8,128)} %copy.18, f32[16,1408]{0,1:T(8,128)S(1)} %copy.17), kind=kLoop, calls=%fused_computation.2 | loop fusion | flops 11534336 | bytes 34693120 | tf_op jit(solution)/shard_map/convert_element_type | solution.py:15
  94.4 5.2 %all-to-all-start = ((bf16[16,256,1408]{1,0,2:T(8,128)(2,1)}), bf16[16,256,1408]{1,0,2:T(8,128)(2,1)}, u32[]{:S(2)}, u32[]{:S(2)}) async-start(bf16[16,256,1408]{1,0,2:T(8,128)(2,1)} %divide_convert_fusion.1), calls=%async_computation | async-start | bytes 23068672 | tf_op jit(solution)/shard_map/all_to_all | solution.py:19
  99.7 0.0 copy-start.1
  99.7 23.7 %copy.22 = f32[16,256,1408]{1,0,2:T(8,128)} copy(f32[16,256,1408]{2,1,0:T(8,128)} %param.5) | data formatting | bytes 46137344 | tf_op args[1]
  123.4 0.0 copy-done.1
  123.4 0.3 copy.21
  123.7 0.0 copy-start
  123.7 0.0 copy-start.2
  123.7 14.2 %divide_convert_fusion = bf16[16,256,1408]{1,0,2:T(8,128)(2,1)} fusion(f32[16,256,1408]{1,0,2:T(8,128)} %copy.22, f32[16,1408]{0,1:T(8,128)S(1)} %copy.21), kind=kLoop, calls=%fused_computation | loop fusion | flops 11534336 | bytes 34693120 | tf_op jit(solution)/shard_map/convert_element_type | solution.py:16
  138.0 89.5 %all-to-all-done = bf16[16,256,1408]{1,0,2:T(8,128)(2,1)} async-done(((bf16[16,256,1408]{1,0,2:T(8,128)(2,1)}), bf16[16,256,1408]{1,0,2:T(8,128)(2,1)}, u32[]{:S(2)}, u32[]{:S(2)}) %all-to-all-start) | async-done | bytes 11534368 | tf_op jit(solution)/shard_map/all_to_all | solution.py:19
  227.4 5.3 %all-to-all-start.1 = ((bf16[16,256,1408]{1,0,2:T(8,128)(2,1)}), bf16[16,256,1408]{1,0,2:T(8,128)(2,1)}, u32[]{:S(2)}, u32[]{:S(2)}) async-start(bf16[16,256,1408]{1,0,2:T(8,128)(2,1)} %divide_convert_fusion), calls=%async_computation.1 | async-start | bytes 23068672 | tf_op jit(solution)/shard_map/all_to_all | solution.py:20
  232.7 0.0 copy-done
  232.7 0.0 copy-done.2
  232.7 0.4 collective-permute-start
  233.2 126.8 %collective-permute-done = bf16[256,16]{0,1:T(8,128)(2,1)S(1)} collective-permute-done((bf16[256,16]{0,1:T(8,128)(2,1)S(1)}, bf16[256,16]{0,1:T(8,128)(2,1)S(1)}, u32[]{:S(2)}, u32[]{:S(2)}) %collective-permute-start) | collective-permute-done | bytes 8224 | tf_op jit(solution)/shard_map/ppermute | solution.py:32
  360.0 0.0 collective-permute-start.1
  360.0 4.0 collective-permute-done.1
  363.9 0.0 collective-permute-start.2
  363.9 4.0 collective-permute-done.2
  367.9 0.0 collective-permute-start.3
  367.9 4.0 collective-permute-done.3
  371.9 0.0 collective-permute-start.4
  371.9 4.0 collective-permute-done.4
  375.9 0.0 collective-permute-start.5
  375.9 4.0 collective-permute-done.5
  379.8 0.0 collective-permute-start.6
  379.8 4.0 collective-permute-done.6
  384.0 14.4 %all_gather.3 = bf16[2048,64]{0,1:T(8,128)(2,1)S(1)} all-gather(bf16[2048,16]{0,1:T(8,128)(2,1)S(1)} %constant_dynamic-slice_fusion), channel_id=1, replica_groups=mesh['expert'=4,'shard'=8] {'expert'}, dimensions={1}, use_global_device_ids=true | all-gather | bytes 327680 | tf_op jit(solution)/shard_map/all_gather | solution.py:36
  398.4 0.7 constant_dynamic-slice_fusion.2
  399.1 0.7 constant_dynamic-slice_fusion.1
  399.7 11.3 %copy.20 = bf16[16,8,256,176]{2,1,3,0:T(8,128)(2,1)} copy(bf16[16,8,256,176]{2,0,3,1:T(8,128)(2,1)} %bitcast.2) | data formatting | bytes 23068672 | tf_op jit(solution)/shard_map/all_to_all | solution.py:19
  411.1 18.0 %all_to_all.29 = bf16[16,2048,176]{1,2,0:T(8,128)(2,1)} reshape(bf16[16,8,256,176]{2,1,3,0:T(8,128)(2,1)} %copy.20) | data formatting | bytes 23068672 | tf_op jit(solution)/shard_map/all_to_all | solution.py:19
  429.0 0.0 all-to-all-done.1
  429.0 11.4 %copy.24 = bf16[16,8,256,176]{2,1,3,0:T(8,128)(2,1)} copy(bf16[16,8,256,176]{2,0,3,1:T(8,128)(2,1)} %bitcast.5) | data formatting | bytes 23068672 | tf_op jit(solution)/shard_map/all_to_all | solution.py:20
  440.4 18.0 %all_to_all.33 = bf16[16,2048,176]{1,2,0:T(8,128)(2,1)} reshape(bf16[16,8,256,176]{2,1,3,0:T(8,128)(2,1)} %copy.24) | data formatting | bytes 23068672 | tf_op jit(solution)/shard_map/all_to_all | solution.py:20
  458.4 0.7 copy.45
  (19 shorter events, 0.1 us)
Async XLA Ops:
  7.2 71.9 %all-reduce.3.cloned.1.call-start = ((), (), s32[]{:S(2)}) async-start(), calls=%async_computation.2 | async-start | bytes 360448 | tf_op jit(solution)/shard_map/psum | solution.py:8
  94.4 133.0 %all-to-all-start = ((bf16[16,256,1408]{1,0,2:T(8,128)(2,1)}), bf16[16,256,1408]{1,0,2:T(8,128)(2,1)}, u32[]{:S(2)}, u32[]{:S(2)}) async-start(bf16[16,256,1408]{1,0,2:T(8,128)(2,1)} %divide_convert_fusion.1), calls=%async_computation | async-start | bytes 23068672 | tf_op jit(solution)/shard_map/all_to_all | solution.py:19
  99.7 23.7 %copy-start.1 = (f32[16,1408]{1,0:T(8,128)S(1)}, f32[16,1408]{1,0:T(8,128)}, u32[]{:S(2)}) copy-start(f32[16,1408]{1,0:T(8,128)} %get-tuple-element.6) | copy-start | bytes 270340
  123.7 109.0 %copy-start = (f32[256,16]{0,1:T(8,128)S(1)}, f32[256,16]{0,1:T(8,128)}, u32[]{:S(2)}) copy-start(f32[256,16]{0,1:T(8,128)} %param.6) | copy-start | bytes 49156
  123.7 109.0 %copy-start.2 = (f32[256]{0:T(256)S(1)}, f32[256]{0:T(256)}, u32[]{:S(2)}) copy-start(f32[256]{0:T(256)} %param.7) | copy-start | bytes 3076
  227.4 201.6 %all-to-all-start.1 = ((bf16[16,256,1408]{1,0,2:T(8,128)(2,1)}), bf16[16,256,1408]{1,0,2:T(8,128)(2,1)}, u32[]{:S(2)}, u32[]{:S(2)}) async-start(bf16[16,256,1408]{1,0,2:T(8,128)(2,1)} %divide_convert_fusion), calls=%async_computation.1 | async-start | bytes 23068672 | tf_op jit(solution)/shard_map/all_to_all | solution.py:20
  232.7 127.2 %collective-permute-start = (bf16[256,16]{0,1:T(8,128)(2,1)S(1)}, bf16[256,16]{0,1:T(8,128)(2,1)S(1)}, u32[]{:S(2)}, u32[]{:S(2)}) collective-permute-start(bf16[256,16]{0,1:T(8,128)(2,1)S(1)} %multiply_convert_fusion), channel_id=1, source_target_pairs={{0,1},{1,2},{2,3},{3,4},{4,5},{5,6},{6,7},{7,0},{8,9},{9,10},{10,1... | collective-permute-start | bytes 24584 | tf_op jit(solution)/shard_map/ppermute | solution.py:32
  360.0 4.0 collective-permute-start.1
  363.9 4.0 collective-permute-start.2
  367.9 4.0 collective-permute-start.3
  371.9 4.0 collective-permute-start.4
  375.9 4.0 collective-permute-start.5
  379.8 4.0 collective-permute-start.6
Sparse Core Ops, SparseCore 0:
  23.2 55.8 all-reduce.2
